TPU v7x, 256 devices: a whole 4x4x8 slice. The times are simulated.
256 devices in a mesh: dap: 16 (over x, z_lo), cplx: 16 (over y, z_hi, core).
Axes of the slice: x: 4, y: 4, z: 8 (z_hi: 2, z_lo: 4; z = z_hi * 4 + z_lo), core: 2. Of those that a mesh axis runs over, the one named last changes fastest.
Arguments:
- pair: bfloat16 [192, 3072, 128], P('dap', 'cplx'), parts along dimension 1, may hold values from -6 to 6
- cotangent: bfloat16 [192, 3072, 128], P('dap', 'cplx'), parts along dimension 1, may hold values from -6 to 6
- residue_mask: int32 [3072], P('cplx'), parts along dimension 0, may hold values 0 or 1
- chain_ids: int32 [3072], P('cplx'), parts along dimension 0, may hold values from 0 to 2, never falling along the last dimension, each value on 1 to 96 neighbouring positions
- chain_embed: float32 [2, 128], replicated, may hold values from -4 to 4
- out_norm_gain: float32 [128], replicated, may hold values from 0.25 to 1.75
- out_proj: bfloat16 [128, 512], replicated, may hold values from -0.5 to 0.5
- out_gate: bfloat16 [128, 128], replicated, may hold values from -0.5 to 0.5
- out_mid_gain: float32 [128], replicated, may hold values from 0.25 to 1.75
- out_final: bfloat16 [128, 128], replicated, may hold values from -0.5 to 0.5
- in_norm_gain: float32 [128], replicated, may hold values from 0.25 to 1.75
- in_proj: bfloat16 [128, 512], replicated, may hold values from -0.5 to 0.5
- in_gate: bfloat16 [128, 128], replicated, may hold values from -0.5 to 0.5
- in_mid_gain: float32 [128], replicated, may hold values from 0.25 to 1.75
- in_final: bfloat16 [128, 128], replicated, may hold values from -0.5 to 0.5
Outputs:
- pair_grad: bfloat16 [192, 3072, 128], P('dap', 'cplx'), parts along dimension 1
- grad_proj: float32 [2048, 512], P('cplx'), parts along dimension 0
- grad_gate: float32 [2048, 128], P('cplx'), parts along dimension 0
- grad_final: float32 [2048, 128], P('cplx'), parts along dimension 0
- grad_norm_gain: float32 [2048], P('cplx'), parts along dimension 0
- grad_mid_gain: float32 [2048], P('cplx'), parts along dimension 0
There are 16 independent parts, one for each index of `cplx`. A program takes and returns all parts, laid end to end along the dimension named above; an argument that names none is the same for every part. Nothing has to cross between parts.
Inputs may be any that keep to these rules, and one draw needn't show every extreme that they name: `chain_ids`: chain numbers never fall along the residues; each chain has at most 96 residues.
All inputs are finite; a program needn't handle non-finite values.
Results may differ from a plain program's by a relative error of at most 0.019.
Values may be sent and summed in bfloat16 or wider, within the bound.
No kernel may reach another device: no remote copies, remote signals or barrier semaphores. Data moves between devices by JAX's collectives and lax.ppermute only.
A program may use at most 128 MiB of HBM per device.

v0:
```python
import jax
import jax.numpy as jnp
from jax import lax
from jax.sharding import PartitionSpec as P


def together(arrays, axis):
    ends = [0]
    for a in arrays:
        ends.append(ends[-1] + a.size)
    subtotal = lax.psum(jnp.concatenate([a.ravel() for a in arrays]), axis)
    return tuple((subtotal[b:e].reshape(a.shape) for a, b, e in zip(arrays, ends, ends[1:])))


def layer_norm(values_in, gain):
    average = jnp.mean(values_in, axis=-1, keepdims=True)
    centred = values_in - average
    variance = jnp.mean(centred * centred, axis=-1, keepdims=True)
    return centred * lax.rsqrt(variance + 1e-05) * gain


def gated_pair(projected, pair_mask, hidden_width):
    masked = pair_mask[..., None]
    left_act = (
        masked
        * jax.nn.sigmoid(projected[..., :hidden_width])
        * projected[..., hidden_width : 2 * hidden_width]
    )
    right_act = (
        masked
        * jax.nn.sigmoid(projected[..., 2 * hidden_width : 3 * hidden_width])
        * projected[..., 3 * hidden_width :]
    )
    return (left_act, right_act)


def shards(
    pair,
    cotangent,
    residue_mask,
    chain_ids,
    chain_embed,
    out_norm_gain,
    out_proj,
    out_gate,
    out_mid_gain,
    out_final,
    in_norm_gain,
    in_proj,
    in_gate,
    in_mid_gain,
    in_final,
):
    f32 = jnp.float32
    bf16 = jnp.bfloat16
    row_count = pair.shape[0]
    res_count = pair.shape[1]
    hidden_width = out_final.shape[0]
    inv_count = 1.0 / res_count
    row_start = lax.axis_index("dap") * row_count
    row_mask = lax.dynamic_slice_in_dim(residue_mask, row_start, row_count, 0)
    row_chain = lax.dynamic_slice_in_dim(chain_ids, row_start, row_count, 0)
    pair_mask = (row_mask[:, None] * residue_mask[None, :]).astype(f32)
    same_chain = row_chain[:, None] == chain_ids[None, :]
    start = pair.astype(f32) + jnp.where(same_chain[..., None], chain_embed[1], chain_embed[0])
    out_normed = layer_norm(start, out_norm_gain).astype(bf16)
    projected = jnp.dot(out_normed, out_proj, preferred_element_type=f32)
    left_act, right_act = gated_pair(projected, pair_mask, hidden_width)
    left_b = left_act.astype(bf16)
    right_b = right_act.astype(bf16)
    x_out = jnp.einsum(
        "ikc,jkc->ijc",
        left_b,
        lax.all_gather(right_b, "dap", axis=0, tiled=True),
        preferred_element_type=f32,
    )
    y_out = layer_norm(x_out, out_mid_gain).astype(bf16)
    update = jax.nn.sigmoid(jnp.dot(out_normed, out_gate, preferred_element_type=f32)) * jnp.dot(
        y_out, out_final, preferred_element_type=f32
    )
    pair_mid = (start + update).astype(bf16)
    mid_f32 = pair_mid.astype(f32)
    normed_f32, norm_back = jax.vjp(layer_norm, mid_f32, in_norm_gain)
    in_normed = normed_f32.astype(bf16)
    proj_in = jnp.dot(in_normed, in_proj, preferred_element_type=f32)
    (left_in, right_in), glu_back = jax.vjp(
        lambda proj_val: gated_pair(proj_val, pair_mask, hidden_width), proj_in
    )
    left_ib = left_in.astype(bf16)
    right_ib = right_in.astype(bf16)
    columns = lax.all_to_all(left_ib, "dap", split_axis=1, concat_axis=0, tiled=True)
    left_block = columns
    x_in = jnp.einsum(
        "kic,kjc->ijc",
        left_block,
        lax.all_gather(right_ib, "dap", axis=0, tiled=True),
        preferred_element_type=f32,
    )
    y_f32, mid_back = jax.vjp(layer_norm, x_in, in_mid_gain)
    y_in = y_f32.astype(bf16)
    logit = jnp.dot(in_normed, in_gate, preferred_element_type=f32)
    value = jnp.dot(y_in, in_final, preferred_element_type=f32)
    sigma = jax.nn.sigmoid(logit)
    upstream = cotangent.astype(f32)
    grad_value = (upstream * sigma).astype(bf16)
    grad_logit = (upstream * value * sigma * (1.0 - sigma)).astype(bf16)
    grad_final = jnp.einsum("ijc,ijd->cd", y_in, grad_value, preferred_element_type=f32) * inv_count
    grad_gate = (
        jnp.einsum("ijc,ijd->cd", in_normed, grad_logit, preferred_element_type=f32) * inv_count
    )
    grad_y = jnp.dot(grad_value, in_final.T, preferred_element_type=f32)
    grad_x, grad_mid = mid_back(grad_y)
    grad_x_b = grad_x.astype(bf16)
    shard_rows = lax.all_gather(grad_x_b, "dap", axis=0, tiled=True)
    left_block = left_ib
    grad_right = jnp.einsum("kic,ijc->kjc", left_block, shard_rows, preferred_element_type=f32)
    new_block = jnp.einsum("kjc,ijc->kic", right_ib, shard_rows, preferred_element_type=f32)
    grad_p = glu_back((new_block, grad_right))[0].astype(bf16)
    grad_proj = jnp.einsum("ijc,ijd->cd", in_normed, grad_p, preferred_element_type=f32) * inv_count
    grad_normed = jnp.dot(grad_p, in_proj.T, preferred_element_type=f32) + jnp.dot(
        grad_logit, in_gate.T, preferred_element_type=f32
    )
    grad_z, grad_norm = norm_back(grad_normed)
    pair_grad = (upstream + grad_z).astype(bf16)
    reduced = tuple(
        (
            part.astype(jnp.float32)
            for part in together(
                (
                    grad_proj.astype(jnp.bfloat16),
                    grad_gate.astype(jnp.bfloat16),
                    grad_final.astype(jnp.bfloat16),
                    (grad_norm * inv_count).astype(jnp.bfloat16),
                    (grad_mid * inv_count).astype(jnp.bfloat16),
                ),
                "dap",
            )
        )
    )
    return (pair_grad, reduced[0], reduced[1], reduced[2], reduced[3], reduced[4])


def solution(mesh):
    placed = (
        P("dap", "cplx", None),
        P("dap", "cplx", None),
        P("cplx"),
        P("cplx"),
        P(),
        P(),
        P(),
        P(),
        P(),
        P(),
        P(),
        P(),
        P(),
        P(),
        P(),
    )
    return jax.shard_map(
        shards,
        mesh=mesh,
        in_specs=placed,
        out_specs=(
            P("dap", "cplx", None),
            P("cplx", None),
            P("cplx", None),
            P("cplx", None),
            P("cplx"),
            P("cplx"),
        ),
        check_vma=False,
    )
```

profile of v0, /device:TPU:8, one launch (start us, length us, event | category | flops | bytes accessed | tf_op | source)
XLA Modules:
  0.0 931.0 jit_solution(3358620269729586650)
XLA Ops:
  11.6 2.3 multiply_reduce_fusion.4
  18.7 2.8 fusion.12
  21.5 204.8 %all-gather.4.cloned.1.call-done = bf16[192,192,128]{2,1,0:T(8,128)(2,1)} async-done(((bf16[12,192,128]{2,1,0:T(8,128)(2,1)}), bf16[192,192,128]{2,1,0:T(8,128)(2,1)}) %all-gather.4.cloned.1.call-update) | async-done | bytes 9437200 | tf_op jit(solution)/shard_map/all_gather | solution.py:74
  226.2 17.4 %copy.46 = bf16[192,192,128]{1,0,2:T(8,128)(2,1)} copy(bf16[192,192,128]{2,1,0:T(8,128)(2,1)} %all-gather.4.cloned.1.call-done) | data formatting | bytes 18874368 | tf_op jit(solution)/shard_map/all_gather | solution.py:74
  243.6 8.2 bitcast_reduce_fusion
  260.7 4.3 all-to-all-start
  266.1 41.9 %all-to-all-done = bf16[12,192,128]{2,0,1:T(8,128)(2,1)} async-done(((bf16[12,192,128]{2,0,1:T(8,128)(2,1)}), bf16[12,192,128]{2,0,1:T(8,128)(2,1)}, u32[]{:S(2)}, u32[]{:S(2)}) %all-to-all-start) | async-done | bytes 589856 | tf_op jit(solution)/shard_map/all_to_all | solution.py:91
  312.1 163.0 %all-gather.6.cloned.1.call-done = bf16[192,192,128]{2,1,0:T(8,128)(2,1)} async-done(((bf16[12,192,128]{2,1,0:T(8,128)(2,1)}), bf16[192,192,128]{2,1,0:T(8,128)(2,1)}) %all-gather.6.cloned.1.call-update) | async-done | bytes 9437200 | tf_op jit(solution)/shard_map/all_gather | solution.py:96
  475.0 17.4 %copy.52 = bf16[192,192,128]{1,0,2:T(8,128)(2,1)} copy(bf16[192,192,128]{2,1,0:T(8,128)(2,1)} %all-gather.6.cloned.1.call-done) | data formatting | bytes 18874368 | tf_op jit(solution)/shard_map/all_gather | solution.py:96
  492.4 7.6 fusion.82
  500.1 2.2 copy.54
  506.4 2.3 add_convert_fusion.1
  509.1 2.6 copy.59
  511.7 2.6 copy.56
  514.3 2.7 fusion.15
  517.0 198.6 %all-gather.8.cloned.1.call-done = bf16[192,192,128]{2,1,0:T(8,128)(2,1)} async-done(((bf16[12,192,128]{2,1,0:T(8,128)(2,1)}), bf16[192,192,128]{2,1,0:T(8,128)(2,1)}) %all-gather.8.cloned.1.call-update) | async-done | bytes 9437200 | tf_op jit(solution)/shard_map/all_gather | solution.py:114
  715.6 17.4 %copy.55 = bf16[192,192,128]{1,0,2:T(8,128)(2,1)} copy(bf16[192,192,128]{2,1,0:T(8,128)(2,1)} %all-gather.8.cloned.1.call-done) | data formatting | bytes 18874368 | tf_op jit(solution)/shard_map/all_gather | solution.py:114
  733.0 9.5 %fusion.84 = f32[128,192,12]{1,2,0:T(8,128)} fusion(bf16[192,192,128]{1,0,2:T(8,128)(2,1)} %copy.55, bf16[12,192,128]{1,0,2:T(8,128)(2,1)} %copy.59), kind=kOutput, calls=%fused_computation.145 | convolution fusion | flops 113246208 | bytes 11206656 | tf_op jit(solution)/shard_map/kjc,ijc->kic/dot_general | solution.py:117
  742.5 2.7 copy.60
  745.2 7.9 fusion.83
  753.1 2.7 copy.57
  755.8 3.7 bitcast_multiply_fusion.3
  767.7 2.5 fusion.22
  770.2 149.9 %all-reduce.6.cloned.1.call-done = bf16[98560]{0:T(1024)(128)(2,1)} async-done(((bf16[98560]{0:T(1024)(128)(2,1)}), bf16[98560]{0:T(1024)(128)(2,1)}) %all-reduce.6.cloned.1.call-update) | async-done | bytes 197136 | tf_op jit(solution)/shard_map/psum | solution.py:11
  (98 shorter events, 39.8 us)
Async XLA Ops:
  7.2 249.1 %copy-start = (bf16[128,512]{1,0:T(8,128)(2,1)S(1)}, bf16[128,512]{1,0:T(8,128)(2,1)}, u32[]{:S(2)}) copy-start(bf16[128,512]{1,0:T(8,128)(2,1)} %param.26) | copy-start | bytes 393220
  7.2 6.9 copy-start.5
  7.2 6.7 copy-start.16
  7.2 6.8 copy-start.18
  7.2 6.8 copy-start.11
  7.2 219.0 %all-gather.4.cloned.1.call-start = ((), (), s32[]{:S(2)}) async-start(), calls=%async_computation.1 | async-start | bytes 10027008 | tf_op jit(solution)/shard_map/all_gather | solution.py:74
  16.7 2.0 copy-start.19
  16.7 458.3 %all-gather.6.cloned.1.call-start = ((), (), s32[]{:S(2)}) async-start(), calls=%async_computation.2 | async-start | bytes 10027008 | tf_op jit(solution)/shard_map/all_gather | solution.py:96
  251.8 0.7 copy-start.17
  252.5 1.3 copy-start.8
  252.5 1.3 copy-start.12
  253.8 2.5 copy-start.15
  257.1 2.3 copy-start.1
  259.4 1.3 copy-start.6
  259.4 5.8 copy-start.13
  260.7 47.2 %all-to-all-start = ((bf16[12,192,128]{2,0,1:T(8,128)(2,1)}), bf16[12,192,128]{2,0,1:T(8,128)(2,1)}, u32[]{:S(2)}, u32[]{:S(2)}) async-start(bf16[12,192,128]{2,0,1:T(8,128)(2,1)} %copy.49), calls=%async_computation | async-start | bytes 1572864 | tf_op jit(solution)/shard_map/all_to_all | solution.py:91
  265.0 450.6 %all-gather.8.cloned.1.call-start = ((), (), s32[]{:S(2)}) async-start(), calls=%async_computation.3 | async-start | bytes 10027008 | tf_op jit(solution)/shard_map/all_gather | solution.py:114
  502.3 1.1 copy-start.2
  502.3 1.1 copy-start.10
  502.3 1.0 copy-start.14
  508.8 411.3 %all-reduce.6.cloned.1.call-start = ((), (), s32[]{:S(2)}) async-start(), calls=%async_computation.4 | async-start | bytes 397312 | tf_op jit(solution)/shard_map/psum | solution.py:11
  760.8 1.1 copy-start.7
  761.6 1.2 copy-start.3
  764.8 2.9 copy-start.4
  (1 other events, 0.7 us)
Sparse Core Ops, SparseCore 0:
  16.8 209.3 all-gather.3
  259.5 215.4 all-gather.5
  508.9 206.6 all-gather.7
  767.8 152.2 all-reduce.5
where the time goes:
time: 933 us; the launch traced here: 931 us
  waiting for transfers between devices  758 us (81%)
  local copies, waits for them, and re-layouts  78.5 us (8%)
  matrix products  49.2 us (5%)
  other arithmetic  26.1 us (3%)
  between operations  14.2 us (2%)
    all_gather x1, waiting for transfers between devices, shards(): lax.all_gather(right_b, 'dap', axis=0, tiled=True)  205 us
    all_gather x1, waiting for transfers between devices, shards(): shard_rows = lax.all_gather(grad_x_b, 'dap', axis=0, tiled=True)  199 us
    all_gather x1, waiting for transfers between devices, shards(): lax.all_gather(right_ib, 'dap', axis=0, tiled=True)  163 us
    psum x1, waiting for transfers between devices, together(): subtotal = lax.psum(jnp.concatenate([a.ravel() for a in arrays]), axis)  150 us
    all_to_all x1, waiting for transfers between devices, shards(): lax.all_to_all(left_ib, 'dap', split_axis=1, concat_axis=0, tiled=True)  41.9 us
  transfers between devices with their start and end apart: 5, of which 5 were waited for; matrix products, arithmetic and copies ran while one was open for 2% of the time, Pallas kernels for 0%

commit v1 on v0

--- a/solution.py
+++ b/solution.py
@@ -2,6 +2,11 @@
 import jax.numpy as jnp
 from jax import lax
 from jax.sharding import PartitionSpec as P
+
+
+def gather_over(array, name, d):
+    outgoing = jnp.stack([array] * lax.axis_size(name))
+    return jnp.concatenate(lax.all_to_all(outgoing, name, 0, 0), axis=d)
 
 
 def together(arrays, axis):
@@ -91,10 +96,7 @@
     columns = lax.all_to_all(left_ib, "dap", split_axis=1, concat_axis=0, tiled=True)
     left_block = columns
     x_in = jnp.einsum(
-        "kic,kjc->ijc",
-        left_block,
-        lax.all_gather(right_ib, "dap", axis=0, tiled=True),
-        preferred_element_type=f32,
+        "kic,kjc->ijc", left_block, gather_over(right_ib, "dap", 0), preferred_element_type=f32
     )
     y_f32, mid_back = jax.vjp(layer_norm, x_in, in_mid_gain)
     y_in = y_f32.astype(bf16)

time: 933 us -> 961 us (1.030)
  blocking collectives: 0 us -> 25.5 us
    all_gather x1 -> x0, waiting for transfers between devices: 163 us -> none  [shards(): lax.all_gather(right_ib, 'dap', axis=0, tiled=True)]
    all_to_all x1, waiting for transfers between devices: 41.9 us -> 202 us  [gather_over(): return jnp.concatenate(lax.all_to_all(outgoing, name, 0, 0), axis=d)]
    all_to_all x0 -> x1, blocking collectives: none -> 25.5 us  [shards(): lax.all_to_all(left_ib, 'dap', split_axis=1, concat_axis=0, tiled=True)]
    all_gather x1 -> x0, local copies, waits for them, and re-layouts: 17.4 us -> none  [shards(): lax.all_gather(right_ib, 'dap', axis=0, tiled=True)]
    reshape x0 -> x1, local copies, waits for them, and re-layouts: none -> 17.4 us  [gather_over(): return jnp.concatenate(lax.all_to_all(outgoing, name, 0, 0), axis=d)]
  transfers between devices with their start and end apart: 5 -> 4, of which waited for: 5 -> 4; matrix products, arithmetic and copies ran while one was open for 2% -> 2% of each run, Pallas kernels for 0% -> 0%
where the time goes in v1:
time: 961 us; the launch traced here: 960 us
  waiting for transfers between devices  755 us (79%)
  local copies, waits for them, and re-layouts  85.4 us (9%)
  matrix products  49.3 us (5%)
  blocking collectives  25.5 us (3%)
  other arithmetic  24.9 us (3%)
  between operations  14.2 us (1%)
    all_gather x1, waiting for transfers between devices, shards(): lax.all_gather(right_b, 'dap', axis=0, tiled=True)  205 us
    all_to_all x1, waiting for transfers between devices, gather_over(): return jnp.concatenate(lax.all_to_all(outgoing, name, 0, 0), axis=d)  202 us
    all_gather x1, waiting for transfers between devices, shards(): shard_rows = lax.all_gather(grad_x_b, 'dap', axis=0, tiled=True)  198 us
    psum x1, waiting for transfers between devices, together(): subtotal = lax.psum(jnp.concatenate([a.ravel() for a in arrays]), axis)  150 us
    all_to_all x1, blocking collectives, shards(): lax.all_to_all(left_ib, 'dap', split_axis=1, concat_axis=0, tiled=True)  25.5 us
  transfers between devices with their start and end apart: 4, of which 4 were waited for; matrix products, arithmetic and copies ran while one was open for 2% of the time, Pallas kernels for 0%

profile of v1, /device:TPU:8, one launch (start us, length us, event | category | flops | bytes accessed | tf_op | source)
XLA Modules:
  0.0 959.7 jit_solution(17594330987696849800)
XLA Ops:
  11.6 2.3 multiply_reduce_fusion.4
  18.7 2.8 fusion.12
  21.5 204.8 %all-gather.3.cloned.1.call-done = bf16[192,192,128]{2,1,0:T(8,128)(2,1)} async-done(((bf16[12,192,128]{2,1,0:T(8,128)(2,1)}), bf16[192,192,128]{2,1,0:T(8,128)(2,1)}) %all-gather.3.cloned.1.call-update) | async-done | bytes 9437200 | tf_op jit(solution)/shard_map/all_gather | solution.py:79
  226.2 17.4 %copy.46 = bf16[192,192,128]{1,0,2:T(8,128)(2,1)} copy(bf16[192,192,128]{2,1,0:T(8,128)(2,1)} %all-gather.3.cloned.1.call-done) | data formatting | bytes 18874368 | tf_op jit(solution)/shard_map/all_gather | solution.py:79
  243.6 8.2 bitcast_reduce_fusion
  259.6 25.5 %all_to_all.23 = bf16[12,192,128]{2,0,1:T(8,128)(2,1)S(1)} all-to-all(bf16[12,192,128]{2,0,1:T(8,128)(2,1)S(1)} %copy.49), channel_id=1, replica_groups=mesh['dap'=16,'cplx'=16] {'dap'}, dimensions={1} | all-to-all | bytes 1179648 | tf_op jit(solution)/shard_map/all_to_all | solution.py:96
  285.1 6.0 stack.2
  291.1 4.9 all-to-all-start
  302.0 202.1 %all-to-all-done = bf16[16,12,192,128]{3,2,1,0:T(8,128)(2,1)} async-done(((bf16[16,12,192,128]{3,2,1,0:T(8,128)(2,1)}), bf16[16,12,192,128]{3,2,1,0:T(8,128)(2,1)}, u32[]{:S(2)}, u32[]{:S(2)}) %all-to-all-start) | async-done | bytes 9437216 | tf_op jit(solution)/shard_map/all_to_all | solution.py:9
  504.1 17.4 %copy.52 = bf16[192,192,128]{1,0,2:T(8,128)(2,1)} copy(bf16[192,192,128]{2,1,0:T(8,128)(2,1)} %bitcast.9) | data formatting | bytes 18874368 | tf_op jit(solution)/shard_map/reshape | solution.py:9
  521.5 7.7 fusion.82
  535.5 2.3 add_convert_fusion.1
  538.1 2.6 copy.59
  540.7 2.6 copy.56
  543.4 2.8 fusion.15
  546.1 198.1 %all-gather.5.cloned.1.call-done = bf16[192,192,128]{2,1,0:T(8,128)(2,1)} async-done(((bf16[12,192,128]{2,1,0:T(8,128)(2,1)}), bf16[192,192,128]{2,1,0:T(8,128)(2,1)}) %all-gather.5.cloned.1.call-update) | async-done | bytes 9437200 | tf_op jit(solution)/shard_map/all_gather | solution.py:116
  744.2 17.4 %copy.55 = bf16[192,192,128]{1,0,2:T(8,128)(2,1)} copy(bf16[192,192,128]{2,1,0:T(8,128)(2,1)} %all-gather.5.cloned.1.call-done) | data formatting | bytes 18874368 | tf_op jit(solution)/shard_map/all_gather | solution.py:116
  761.6 9.5 fusion.84
  771.1 2.7 copy.60
  773.8 7.9 fusion.83
  781.7 2.7 copy.57
  784.4 3.7 bitcast_multiply_fusion.3
  796.3 2.5 fusion.22
  798.8 150.0 %all-reduce.6.cloned.1.call-done = bf16[98560]{0:T(1024)(128)(2,1)} async-done(((bf16[98560]{0:T(1024)(128)(2,1)}), bf16[98560]{0:T(1024)(128)(2,1)}) %all-reduce.6.cloned.1.call-update) | async-done | bytes 197136 | tf_op jit(solution)/shard_map/psum | solution.py:16
  (99 shorter events, 41.8 us)
Async XLA Ops:
  7.2 249.0 %copy-start = (bf16[128,512]{1,0:T(8,128)(2,1)S(1)}, bf16[128,512]{1,0:T(8,128)(2,1)}, u32[]{:S(2)}) copy-start(bf16[128,512]{1,0:T(8,128)(2,1)} %param.26) | copy-start | bytes 393220
  7.2 6.9 copy-start.5
  7.2 6.7 copy-start.17
  7.2 6.8 copy-start.19
  7.2 6.8 copy-start.12
  7.2 219.0 %all-gather.3.cloned.1.call-start = ((), (), s32[]{:S(2)}) async-start(), calls=%async_computation.2 | async-start | bytes 10027008 | tf_op jit(solution)/shard_map/all_gather | solution.py:79
  16.7 2.0 copy-start.20
  251.8 0.7 copy-start.18
  252.5 1.3 copy-start.9
  252.5 1.3 copy-start.13
  253.7 2.5 copy-start.16
  257.0 2.2 copy-start.1
  259.2 25.9 %copy-start.7 = (bf16[12,192,128]{2,1,0:T(8,128)(2,1)}, bf16[12,192,128]{2,1,0:T(8,128)(2,1)S(1)}, u32[]{:S(2)}) copy-start(bf16[12,192,128]{2,1,0:T(8,128)(2,1)S(1)} %get-tuple-element.18) | copy-start | bytes 1769476
  259.2 25.9 %copy-start.6 = (bf16[12,192,128]{2,1,0:T(8,128)(2,1)}, bf16[12,192,128]{2,1,0:T(8,128)(2,1)S(1)}, u32[]{:S(2)}) copy-start(bf16[12,192,128]{2,1,0:T(8,128)(2,1)S(1)} %get-tuple-element.19) | copy-start | bytes 1769476
  291.1 5.2 copy-start.14
  291.1 213.0 %all-to-all-start = ((bf16[16,12,192,128]{3,2,1,0:T(8,128)(2,1)}), bf16[16,12,192,128]{3,2,1,0:T(8,128)(2,1)}, u32[]{:S(2)}, u32[]{:S(2)}) async-start(bf16[16,12,192,128]{3,2,1,0:T(8,128)(2,1)} %stack.2), calls=%async_computation | async-start | bytes 18874368 | tf_op jit(solution)/shard_map/all_to_all | solution.py:9
  296.0 448.2 %all-gather.5.cloned.1.call-start = ((), (), s32[]{:S(2)}) async-start(), calls=%async_computation.3 | async-start | bytes 10027008 | tf_op jit(solution)/shard_map/all_gather | solution.py:116
  531.4 1.1 copy-start.2
  531.4 1.1 copy-start.11
  531.4 1.0 copy-start.15
  537.8 411.0 %all-reduce.6.cloned.1.call-start = ((), (), s32[]{:S(2)}) async-start(), calls=%async_computation.4 | async-start | bytes 397312 | tf_op jit(solution)/shard_map/psum | solution.py:16
  789.4 1.1 copy-start.8
  790.2 1.3 copy-start.3
  793.4 2.9 copy-start.4
  (1 other events, 0.7 us)
Sparse Core Ops, SparseCore 0:
  16.8 209.3 all-gather.2
  537.9 206.2 all-gather.4
  796.4 152.3 all-reduce.5
